TPU v7x, 1024 devices: a whole 4x8x16 slice. The times are simulated.
1024 devices in a mesh: ctx: 64 (over z, y_lo, core), head: 16 (over y_hi, x).
Axes of the slice: x: 4, y: 8 (y_hi: 4, y_lo: 2; y = y_hi * 2 + y_lo), z: 16, core: 2. Of those that a mesh axis runs over, the one named last changes fastest.
Arguments:
- q_latent: bfloat16 [8192, 128, 512], P('ctx', 'head'), may hold values from -4 to 4
- q_rope: bfloat16 [8192, 8192], P('ctx', 'head'), may hold values from -5 to 5
- latent: bfloat16 [8192, 512], P('ctx'), may hold values from -5 to 5
- key_rope: bfloat16 [8192, 64], P('ctx'), may hold values from -5 to 5
- out_grad: bfloat16 [8192, 128, 512], P('ctx', 'head'), may hold values from -5 to 5
- inputs: bfloat16 [8192, 7168], P('ctx', 'head'), may hold values from -5 to 5
- doc_ids: int32 [8192], replicated, may hold values from 0 to 7, never falling along the last dimension, each value on 1 to 2048 neighbouring positions
Outputs:
- q_latent_grad: bfloat16 [8192, 128, 512], P('ctx', 'head')
- q_rope_grad: bfloat16 [8192, 8192], P('ctx', 'head')
- latent_grad: bfloat16 [8192, 512], P('ctx')
- key_rope_grad: bfloat16 [8192, 64], P('ctx')
- proj_grad: float32 [512, 7168], P('ctx', 'head')
Inputs may be any that keep to these rules, and one draw needn't show every extreme that they name: `doc_ids`: ids never fall along the sequence; each document has at most 2048 positions.
All inputs are finite; a program needn't handle non-finite values.
Results may differ from a plain program's by a relative error of at most 0.0058.
Values may be sent and summed in bfloat16 or wider, within the bound.
A program may use at most 32 MiB of HBM per device.

v0:
```python
import jax
import jax.numpy as jnp
from jax import lax
from jax.sharding import Mesh
from jax.sharding import PartitionSpec as P

WIN_BLK = 3
CTX = ("ctx_0", "ctx_1", "ctx_2")


softmax_scale = 192.0 ** (-0.5)


def passed_along(array, axis, by):
    peers = lax.axis_size(axis)
    pairs = [(i, i + by) for i in range(peers) if 0 <= i + by < peers]
    return lax.ppermute(array, axis, pairs)


def in_blocks(array, dim, peers):
    before, after = (array.shape[:dim], array.shape[dim + 1 :])
    return jnp.moveaxis(array.reshape(*before, peers, -1, *after), dim, 0)


def summed_on_arrival(array, axis, dim):
    peers = lax.axis_size(axis)
    tiles = lax.all_to_all(in_blocks(array, dim, peers), axis, 0, 0, tiled=True)
    return jnp.sum(tiles, axis=0)


def in_one_piece(arrays, axis, dim, along):
    widths = [a.shape[along] for a in arrays]
    both = jnp.concatenate(arrays, axis=along)
    whole = summed_on_arrival(both, axis, dim)
    return tuple(jnp.split(whole, [sum(widths[:k]) for k in range(1, len(widths))], axis=along))


def laid_out(tiles, dim):
    tiles = jnp.moveaxis(tiles, 0, dim)
    dims = tiles.shape
    return tiles.reshape(*dims[:dim], dims[dim] * dims[dim + 1], *dims[dim + 2 :])


def gather_together(arrays, axis, dims):
    ravelled = jnp.concatenate([a.reshape(-1) for a in arrays])
    lines, at, outs = (lax.all_gather(ravelled, axis), 0, [])
    for a, dim in zip(arrays, dims):
        tiles = lines[:, at : at + a.size].reshape(-1, *a.shape)
        outs.append(laid_out(tiles, dim))
        at += a.size
    return tuple(outs)


def reduced_to_own(tiles, axes, order):
    inside = tiles.shape[1:]
    tiles = tiles.reshape(*(lax.axis_size(a) for a in axes), *inside)
    tiles = jnp.moveaxis(tiles, order, range(len(axes))).reshape(-1, *inside)
    for k in order:
        tiles = lax.psum_scatter(tiles, axes[k], scatter_dimension=0, tiled=True)
    return tiles[0]


def scatter_axes(array, axes, order, dim):
    peers = lax.axis_size(axes)
    return reduced_to_own(in_blocks(array, dim, peers), axes, order)


def shards(q_latent, q_rope, latent, key_rope, out_grad, inputs, doc_ids):
    tok = latent.shape[0]
    heads_here = q_latent.shape[1]
    rope_width = key_rope.shape[1]
    lat_width = latent.shape[1]
    depth = WIN_BLK
    window = depth * tok
    rank = lax.axis_index(CTX)
    earlier = []
    for back in range(depth, 0, -1):
        earlier.append(passed_along((latent, key_rope), CTX, back))
    keys_lat = jnp.concatenate([pair[0] for pair in earlier] + [latent], axis=0)
    keys_rope = jnp.concatenate([pair[1] for pair in earlier] + [key_rope], axis=0)
    start = rank * tok
    doc_pad = jnp.concatenate([jnp.full((window,), -1, jnp.int32), doc_ids], axis=0)
    key_doc = lax.dynamic_slice_in_dim(doc_pad, start, window + tok, 0)
    query_doc = lax.dynamic_slice_in_dim(doc_ids, start, tok, 0)
    qpos = jnp.arange(tok, dtype=jnp.int32)
    kpos = jnp.arange(window + tok, dtype=jnp.int32) - window
    allowed = (
        (kpos[None, :] <= qpos[:, None])
        & (qpos[:, None] - kpos[None, :] < window)
        & (key_doc[None, :] == query_doc[:, None])
    )
    qrope_heads = q_rope.reshape(tok, heads_here, rope_width)
    scores = (
        jnp.einsum("thj,kj->thk", q_latent, keys_lat, preferred_element_type=jnp.float32)
        + jnp.einsum("thr,kr->thk", qrope_heads, keys_rope, preferred_element_type=jnp.float32)
    ) * softmax_scale
    masked = jnp.where(allowed[:, None, :], scores, -jnp.inf)
    top = jnp.max(masked, axis=-1, keepdims=True)
    expo = jnp.exp(masked - top)
    probs = expo / jnp.sum(expo, axis=-1, keepdims=True)
    probs_low = probs.astype(jnp.bfloat16)
    merged = jnp.einsum("thk,kj->thj", probs_low, keys_lat, preferred_element_type=jnp.float32)
    delta = jnp.sum(out_grad * merged, axis=-1)
    dprob = jnp.einsum("thj,kj->thk", out_grad, keys_lat, preferred_element_type=jnp.float32)
    dscore = (probs * (dprob - delta[..., None]) * softmax_scale).astype(jnp.bfloat16)
    q_latent_grad = jnp.einsum(
        "thk,kj->thj", dscore, keys_lat, preferred_element_type=jnp.float32
    ).astype(jnp.bfloat16)
    q_rope_grad = jnp.einsum("thk,kr->thr", dscore, keys_rope, preferred_element_type=jnp.float32)
    q_rope_grad = q_rope_grad.reshape(tok, heads_here * rope_width).astype(jnp.bfloat16)
    part_lat = jnp.einsum(
        "thk,thj->kj", dscore, q_latent, preferred_element_type=jnp.float32
    ) + jnp.einsum("thk,thj->kj", probs_low, out_grad, preferred_element_type=jnp.float32)
    part_rope = jnp.einsum("thk,thr->kr", dscore, qrope_heads, preferred_element_type=jnp.float32)
    blocks_lat = part_lat.reshape(depth + 1, tok, lat_width)
    blocks_rope = part_rope.reshape(depth + 1, tok, rope_width)
    share_lat, share_rope = in_one_piece((blocks_lat, blocks_rope), "head", 1, 2)
    own_lat = share_lat[depth]
    own_rope = share_rope[depth]
    for back in range(1, depth + 1):
        got_lat, got_rope = passed_along(
            (share_lat[depth - back], share_rope[depth - back]), CTX, -back
        )
        own_lat = own_lat + got_lat
        own_rope = own_rope + got_rope
    latent_grad, key_rope_grad = gather_together(
        (own_lat.astype(jnp.bfloat16), own_rope.astype(jnp.bfloat16)), "head", (0, 0)
    )
    proj_grad = scatter_axes(
        lax.dot_general(
            latent_grad, inputs, (((0,), (0,)), ((), ())), preferred_element_type=jnp.float32
        ),
        CTX,
        (2, 0, 1),
        0,
    )
    return (q_latent_grad, q_rope_grad, latent_grad, key_rope_grad, proj_grad)


def solution(mesh):
    torus = Mesh(
        mesh.devices.reshape(16, 2, 2, mesh.shape["head"]), ("ctx_0", "ctx_1", "ctx_2", "head")
    )
    placed = (
        P(CTX, "head", None),
        P(CTX, "head"),
        P(CTX, None),
        P(CTX, None),
        P(CTX, "head", None),
        P(CTX, "head"),
        P(),
    )
    return jax.shard_map(
        shards,
        mesh=torus,
        in_specs=placed,
        out_specs=(
            P(CTX, "head", None),
            P(CTX, "head"),
            P(CTX, None),
            P(CTX, None),
            P(CTX, "head"),
        ),
        check_vma=False,
    )
```

profile of v0, /device:TPU:8, one launch (start us, length us, event | category | flops | bytes accessed | tf_op | source)
XLA Modules:
  0.0 286.2 jit_solution(7755149446015016261)
XLA Ops:
  7.2 2.1 collective-permute-start.2
  9.3 4.2 %collective-permute-start.1 = (bf16[128,512]{1,0:T(8,128)(2,1)}, bf16[128,512]{1,0:T(8,128)(2,1)S(1)}, u32[]{:S(2)}, u32[]{:S(2)}) collective-permute-start(bf16[128,512]{1,0:T(8,128)(2,1)} %param.9), channel_id=1, source_target_pairs={{0,32},{16,48},{32,64},{48,80},{64,96},{80,112},{96,128},{112,144}... | collective-permute-start | bytes 393224 | tf_op jit(solution)/shard_map/ppermute | solution.py:17
  13.5 3.3 %collective-permute-start.5 = (bf16[128,64]{0,1:T(8,128)(2,1)}, bf16[128,64]{0,1:T(8,128)(2,1)S(1)}, u32[]{:S(2)}, u32[]{:S(2)}) collective-permute-start(bf16[128,64]{0,1:T(8,128)(2,1)} %param.10), channel_id=1, source_target_pairs={{0,16},{16,32},{32,48},{48,64},{64,80},{80,96},{96,112},{112,128},... | collective-permute-start | bytes 49160 | tf_op jit(solution)/shard_map/ppermute | solution.py:17
  16.8 4.2 %collective-permute-start.4 = (bf16[128,64]{0,1:T(8,128)(2,1)}, bf16[128,64]{0,1:T(8,128)(2,1)S(1)}, u32[]{:S(2)}, u32[]{:S(2)}) collective-permute-start(bf16[128,64]{0,1:T(8,128)(2,1)} %param.10), channel_id=1, source_target_pairs={{0,32},{16,48},{32,64},{48,80},{64,96},{80,112},{96,128},{112,144}... | collective-permute-start | bytes 49160 | tf_op jit(solution)/shard_map/ppermute | solution.py:17
  21.0 3.1 %collective-permute-start.3 = (bf16[128,64]{0,1:T(8,128)(2,1)}, bf16[128,64]{0,1:T(8,128)(2,1)S(1)}, u32[]{:S(2)}, u32[]{:S(2)}) collective-permute-start(bf16[128,64]{0,1:T(8,128)(2,1)} %param.10), channel_id=1, source_target_pairs={{0,48},{16,64},{32,80},{48,96},{64,112},{80,128},{96,144},{112,160... | collective-permute-start | bytes 49160 | tf_op jit(solution)/shard_map/ppermute | solution.py:17
  26.0 1.0 copy.58
  27.1 4.4 %collective-permute-start = (bf16[128,512]{1,0:T(8,128)(2,1)}, bf16[128,512]{1,0:T(8,128)(2,1)S(1)}, u32[]{:S(2)}, u32[]{:S(2)}) collective-permute-start(bf16[128,512]{1,0:T(8,128)(2,1)} %param.9), channel_id=1, source_target_pairs={{0,48},{16,64},{32,80},{48,96},{64,112},{80,128},{96,144},{112,160... | collective-permute-start | bytes 393224 | tf_op jit(solution)/shard_map/ppermute | solution.py:17
  31.5 1.2 fusion.23
  32.7 2.3 collective-permute-done
  35.0 1.1 fusion.7
  36.5 0.8 copy-done.3
  37.3 1.2 convolution_bitcast_fusion.1
  38.5 1.2 multiply_reduce_fusion
  39.8 1.4 fusion.6
  42.3 0.9 fusion.10
  43.3 43.3 %all_to_all.5 = f32[16,4,8,576]{3,2,1,0:T(8,128)S(1)} all-to-all(f32[16,4,8,576]{3,2,1,0:T(8,128)S(1)} %copy_bitcast_fusion), channel_id=1, replica_groups=mesh['ctx_0'=16,'ctx_1'=2,'ctx_2'=2,'head'=16] {'head'}, dimensions={0} | all-to-all | bytes 2359296 | tf_op jit(solution)/shard_map/all_to_all | solution.py:27
  86.7 1.3 collective-permute-start.11
  88.0 1.9 collective-permute-start.10
  89.9 1.9 collective-permute-start.9
  91.9 1.3 collective-permute-start.8
  93.2 1.9 collective-permute-start.7
  95.1 1.9 collective-permute-start.6
  97.2 1.4 collective-permute-done.8
  98.6 2.0 collective-permute-done.7
  100.6 41.9 %all-gather.1 = bf16[16,1,4608]{2,1,0:T(2,128)(2,1)S(1)} all-gather(bf16[1,1,4608]{2,1,0:T(2,128)(2,1)S(1)} %reshape.106), channel_id=2, replica_groups=mesh['ctx_0'=16,'ctx_1'=2,'ctx_2'=2,'head'=16] {'head'}, dimensions={0}, use_global_device_ids=true | all-gather | bytes 156672 | tf_op jit(solution)/shard_map/all_gather | solution.py:46
  142.8 1.2 convolution_bitcast_fusion
  144.0 1.1 copy.69
  145.1 29.9 %reduce-scatter.4.cloned.1.call-done = f32[32,8,448]{2,1,0:T(8,128)} async-done(((f32[64,8,448]{2,1,0:T(8,128)}), f32[32,8,448]{2,1,0:T(8,128)}) %reduce-scatter.4.cloned.1.call-update) | async-done | bytes 458768 | tf_op jit(solution)/shard_map/reduce_scatter | solution.py:59
  175.1 1.8 convolution_convert_fusion
  176.9 77.3 %reduce-scatter.6.cloned.1.call-done = f32[2,8,448]{2,1,0:T(8,128)} async-done(((f32[32,8,448]{2,1,0:T(8,128)}), f32[2,8,448]{2,1,0:T(8,128)}) %reduce-scatter.6.cloned.1.call-update) | async-done | bytes 28688 | tf_op jit(solution)/shard_map/reduce_scatter | solution.py:59
  254.6 1.5 copy.70
  257.7 22.0 %reduce-scatter.8.cloned.1.call-done = f32[1,8,448]{2,1,0:T(8,128)} async-done(((f32[2,8,448]{2,1,0:T(8,128)}), f32[1,8,448]{2,1,0:T(8,128)}) %reduce-scatter.8.cloned.1.call-update) | async-done | bytes 14352 | tf_op jit(solution)/shard_map/reduce_scatter | solution.py:59
  (60 shorter events, 6.0 us)
Async XLA Ops:
  7.2 27.8 %copy-start = (bf16[128,8,512]{2,1,0:T(8,128)(2,1)S(1)}, bf16[128,8,512]{2,1,0:T(8,128)(2,1)}, u32[]{:S(2)}) copy-start(bf16[128,8,512]{2,1,0:T(8,128)(2,1)} %param.7) | copy-start | bytes 3145732
  7.2 27.8 %copy-start.4 = (bf16[128,512]{1,0:T(8,128)(2,1)S(1)}, bf16[128,512]{1,0:T(8,128)(2,1)}, u32[]{:S(2)}) copy-start(bf16[128,512]{1,0:T(8,128)(2,1)} %param.9) | copy-start | bytes 393220
  7.2 167.8 %reduce-scatter.4.cloned.1.call-start = ((), (), s32[]{:S(2)}) async-start(), calls=%async_computation.4 | async-start | bytes 1572864 | tf_op jit(solution)/shard_map/reduce_scatter | solution.py:59
  7.2 25.5 %collective-permute-start.2 = (bf16[128,512]{1,0:T(8,128)(2,1)}, bf16[128,512]{1,0:T(8,128)(2,1)S(1)}, u32[]{:S(2)}, u32[]{:S(2)}) collective-permute-start(bf16[128,512]{1,0:T(8,128)(2,1)} %param.9), channel_id=1, source_target_pairs={{0,16},{16,32},{32,48},{48,64},{64,80},{80,96},{96,112},{112,128},... | collective-permute-start | bytes 393224 | tf_op jit(solution)/shard_map/ppermute | solution.py:17
  9.3 23.4 %collective-permute-start.1 = (bf16[128,512]{1,0:T(8,128)(2,1)}, bf16[128,512]{1,0:T(8,128)(2,1)S(1)}, u32[]{:S(2)}, u32[]{:S(2)}) collective-permute-start(bf16[128,512]{1,0:T(8,128)(2,1)} %param.9), channel_id=1, source_target_pairs={{0,32},{16,48},{32,64},{48,80},{64,96},{80,112},{96,128},{112,144}... | collective-permute-start | bytes 393224 | tf_op jit(solution)/shard_map/ppermute | solution.py:17
  13.5 13.6 %collective-permute-start.5 = (bf16[128,64]{0,1:T(8,128)(2,1)}, bf16[128,64]{0,1:T(8,128)(2,1)S(1)}, u32[]{:S(2)}, u32[]{:S(2)}) collective-permute-start(bf16[128,64]{0,1:T(8,128)(2,1)} %param.10), channel_id=1, source_target_pairs={{0,16},{16,32},{32,48},{48,64},{64,80},{80,96},{96,112},{112,128},... | collective-permute-start | bytes 49160 | tf_op jit(solution)/shard_map/ppermute | solution.py:17
  16.8 14.7 %collective-permute-start.4 = (bf16[128,64]{0,1:T(8,128)(2,1)}, bf16[128,64]{0,1:T(8,128)(2,1)S(1)}, u32[]{:S(2)}, u32[]{:S(2)}) collective-permute-start(bf16[128,64]{0,1:T(8,128)(2,1)} %param.10), channel_id=1, source_target_pairs={{0,32},{16,48},{32,64},{48,80},{64,96},{80,112},{96,128},{112,144}... | collective-permute-start | bytes 49160 | tf_op jit(solution)/shard_map/ppermute | solution.py:17
  21.0 10.5 %collective-permute-start.3 = (bf16[128,64]{0,1:T(8,128)(2,1)}, bf16[128,64]{0,1:T(8,128)(2,1)S(1)}, u32[]{:S(2)}, u32[]{:S(2)}) collective-permute-start(bf16[128,64]{0,1:T(8,128)(2,1)} %param.10), channel_id=1, source_target_pairs={{0,48},{16,64},{32,80},{48,96},{64,112},{80,128},{96,144},{112,160... | collective-permute-start | bytes 49160 | tf_op jit(solution)/shard_map/ppermute | solution.py:17
  27.1 7.9 %collective-permute-start = (bf16[128,512]{1,0:T(8,128)(2,1)}, bf16[128,512]{1,0:T(8,128)(2,1)S(1)}, u32[]{:S(2)}, u32[]{:S(2)}) collective-permute-start(bf16[128,512]{1,0:T(8,128)(2,1)} %param.9), channel_id=1, source_target_pairs={{0,48},{16,64},{32,80},{48,96},{64,112},{80,128},{96,144},{112,160... | collective-permute-start | bytes 393224 | tf_op jit(solution)/shard_map/ppermute | solution.py:17
  32.7 7.0 %copy-start.7 = (bf16[128,512]{1,0:T(8,128)(2,1)}, bf16[128,512]{1,0:T(8,128)(2,1)S(1)}, u32[]{:S(2)}) copy-start(bf16[128,512]{1,0:T(8,128)(2,1)S(1)} %collective-permute-done.2) | copy-start | bytes 393220
  32.7 7.0 %copy-start.8 = (bf16[128,512]{1,0:T(8,128)(2,1)}, bf16[128,512]{1,0:T(8,128)(2,1)S(1)}, u32[]{:S(2)}) copy-start(bf16[128,512]{1,0:T(8,128)(2,1)S(1)} %collective-permute-done.1) | copy-start | bytes 393220
  35.0 4.7 %copy-start.9 = (bf16[128,512]{1,0:T(8,128)(2,1)}, bf16[128,512]{1,0:T(8,128)(2,1)S(1)}, u32[]{:S(2)}) copy-start(bf16[128,512]{1,0:T(8,128)(2,1)S(1)} %collective-permute-done) | copy-start | bytes 393220
  36.1 1.2 copy-start.3
  38.5 1.2 copy-start.5
  86.7 8.4 %collective-permute-start.11 = (f32[8,64]{1,0:T(8,128)S(1)}, f32[8,64]{1,0:T(8,128)S(1)}, u32[]{:S(2)}, u32[]{:S(2)}) collective-permute-start(f32[8,64]{1,0:T(8,128)S(1)} %get-tuple-element.29), channel_id=1, source_target_pairs={{48,0},{64,16},{80,32},{96,48},{112,64},{128,80},{144,96},{160,112... | collective-permute-start | bytes 6152 | tf_op jit(solution)/shard_map/ppermute | solution.py:17
  88.0 9.0 %collective-permute-start.10 = (f32[8,64]{1,0:T(8,128)S(1)}, f32[8,64]{1,0:T(8,128)S(1)}, u32[]{:S(2)}, u32[]{:S(2)}) collective-permute-start(f32[8,64]{1,0:T(8,128)S(1)} %get-tuple-element.30), channel_id=1, source_target_pairs={{32,0},{48,16},{64,32},{80,48},{96,64},{112,80},{128,96},{144,112}... | collective-permute-start | bytes 6152 | tf_op jit(solution)/shard_map/ppermute | solution.py:17
  89.9 7.1 %collective-permute-start.9 = (f32[8,64]{1,0:T(8,128)S(1)}, f32[8,64]{1,0:T(8,128)S(1)}, u32[]{:S(2)}, u32[]{:S(2)}) collective-permute-start(f32[8,64]{1,0:T(8,128)S(1)} %get-tuple-element.28), channel_id=1, source_target_pairs={{16,0},{32,16},{48,32},{64,48},{80,64},{96,80},{112,96},{128,112},... | collective-permute-start | bytes 6152 | tf_op jit(solution)/shard_map/ppermute | solution.py:17
  91.9 6.7 %collective-permute-start.8 = (f32[8,512]{1,0:T(8,128)S(1)}, f32[8,512]{1,0:T(8,128)S(1)}, u32[]{:S(2)}, u32[]{:S(2)}) collective-permute-start(f32[8,512]{1,0:T(8,128)S(1)} %get-tuple-element.26), channel_id=1, source_target_pairs={{48,0},{64,16},{80,32},{96,48},{112,64},{128,80},{144,96},{160,112... | collective-permute-start | bytes 49160 | tf_op jit(solution)/shard_map/ppermute | solution.py:17
  93.2 7.4 %collective-permute-start.7 = (f32[8,512]{1,0:T(8,128)S(1)}, f32[8,512]{1,0:T(8,128)S(1)}, u32[]{:S(2)}, u32[]{:S(2)}) collective-permute-start(f32[8,512]{1,0:T(8,128)S(1)} %get-tuple-element.27), channel_id=1, source_target_pairs={{32,0},{48,16},{64,32},{80,48},{96,64},{112,80},{128,96},{144,112}... | collective-permute-start | bytes 49160 | tf_op jit(solution)/shard_map/ppermute | solution.py:17
  95.1 5.5 %collective-permute-start.6 = (f32[8,512]{1,0:T(8,128)S(1)}, f32[8,512]{1,0:T(8,128)S(1)}, u32[]{:S(2)}, u32[]{:S(2)}) collective-permute-start(f32[8,512]{1,0:T(8,128)S(1)} %get-tuple-element.25), channel_id=1, source_target_pairs={{16,0},{32,16},{48,32},{64,48},{80,64},{96,80},{112,96},{128,112},... | collective-permute-start | bytes 49160 | tf_op jit(solution)/shard_map/ppermute | solution.py:17
  142.6 2.4 copy-start.1
  144.0 31.1 %copy-start.6 = (bf16[128,512]{1,0:T(8,128)(2,1)S(1)}, bf16[128,512]{1,0:T(8,128)(2,1)}, u32[]{:S(2)}) copy-start(bf16[128,512]{1,0:T(8,128)(2,1)} %param.9) | copy-start | bytes 393220
  145.1 109.2 %copy-start.2 = (bf16[128,64]{0,1:T(8,128)(2,1)S(1)}, bf16[128,64]{0,1:T(8,128)(2,1)}, u32[]{:S(2)}) copy-start(bf16[128,64]{0,1:T(8,128)(2,1)} %param.10) | copy-start | bytes 49156
  145.1 109.1 %reduce-scatter.6.cloned.1.call-start = ((), (), s32[]{:S(2)}) async-start(), calls=%async_computation.5 | async-start | bytes 557056 | tf_op jit(solution)/shard_map/reduce_scatter | solution.py:59
  175.1 104.6 %reduce-scatter.8.cloned.1.call-start = ((), (), s32[]{:S(2)}) async-start(), calls=%async_computation.6 | async-start | bytes 49152 | tf_op jit(solution)/shard_map/reduce_scatter | solution.py:59
Sparse Core Ops, SparseCore 0:
  145.2 29.8 reduce-scatter.3
  178.4 75.7 reduce-scatter.5
  258.1 21.4 reduce-scatter.7
where the time goes:
time: 287 us; the launch traced here: 286 us
  waiting for transfers between devices  135 us (47%)
  blocking collectives  85.2 us (30%)
  starting transfers between devices  31.6 us (11%)
  between operations  14.2 us (5%)
  matrix products  10.6 us (4%)
  local copies, waits for them, and re-layouts  7.19 us (3%)
    reduce_scatter x3, waiting for transfers between devices, reduced_to_own(): tiles = lax.psum_scatter(tiles, axes[k], scatter_dimension=0, tiled=True)  129 us
    all_to_all x1, blocking collectives, summed_on_arrival(): tiles = lax.all_to_all(in_blocks(array, dim, peers), axis, 0, 0, tiled=True)  43.3 us
    all_gather x1, blocking collectives, gather_together(): lines, at, outs = (lax.all_gather(ravelled, axis), 0, [])  41.9 us
    ppermute x12, starting transfers between devices, passed_along(): return lax.ppermute(array, axis, pairs)  31.5 us
  transfers between devices with their start and end apart: 15, of which 6 were waited for; matrix products, arithmetic and copies ran while one was open for 3% of the time, Pallas kernels for 0%

commit v1 on v0

v1 whole, which is shorter than its diff:
```python
import functools

import jax
import jax.numpy as jnp
from jax import lax
from jax.experimental import pallas as pl
from jax.experimental.pallas import tpu as pltpu
from jax.sharding import PartitionSpec as P

MESH = pl.DeviceIdType.MESH
BF16, F32 = jnp.bfloat16, jnp.float32
SCALE = 192.0 ** (-0.5)
FAR = -1e30
EXT = 128
QUAD = 4
SLOTS = 4
NT = (((1,), (1,)), ((), ()))
TN = (((0,), (0,)), ((), ()))


def dot(a, b, dims=(((1,), (0,)), ((), ()))):
    return lax.dot_general(a, b, dims, preferred_element_type=F32)


def iota(shape, dim):
    return lax.broadcasted_iota(jnp.int32, shape, dim)


def kernel(cfg, q_hbm, qr_hbm, lat_hbm, rope_hbm, og_hbm, in_hbm, doc_hbm,
           dq_hbm, dqr_hbm, lg_hbm, krg_hbm, pg_hbm,
           qx, og, qr, keys, rope, inp, doc, perm, st, dt, probs, dscore, part, xbuf, ysend, ybuf,
           gbuf, latp, ebuf, zsend, zbuf, dq, dqr, krx, pg, hot, pick, drop,
           load_sem, hs_sem, hr_sem, xs_sem, xr_sem, ys_sem, yr_sem, gs_sem, gr_sem,
           es_sem, er_sem, is_sem, ir_sem, zs_sem, zr_sem, out_sem):
    n_ctx, n_z, n_yh, n_x, tok, wid, heads = cfg
    rows = tok * heads
    n_head = n_yh * n_x
    full = wid + EXT
    c, h = lax.axis_index("ctx"), lax.axis_index("head")
    z, quad = lax.div(c, QUAD), lax.rem(c, QUAD)
    yh, x = lax.div(h, n_x), lax.rem(h, n_x)
    own = (SLOTS - 1) * tok
    chunks = [(0, wid // 2), (wid // 2, wid // 2), (wid, EXT)]

    def ctx_at(by):
        return lax.rem(c + (by + n_ctx), n_ctx)

    def yh_at(by):
        return lax.rem(yh + by, n_yh)

    def x_at(by):
        return lax.rem(x + by, n_x)

    def quad_at(by):
        return z * QUAD + lax.rem(quad + by, QUAD)

    def z_at(by):
        return lax.rem(z + by, n_z) * QUAD + quad

    def near(ref_a, ref_b, sem):
        return pltpu.make_async_copy(ref_a, ref_b, sem)

    def send(src, dst, ssem, rsem, ci, hi):
        copy = pltpu.make_async_remote_copy(
            src_ref=src, dst_ref=dst, send_sem=ssem, recv_sem=rsem, device_id=(ci, hi), device_id_type=MESH
        )
        copy.start()
        return copy

    barrier = pltpu.get_barrier_semaphore()
    count = 0
    for by in range(-3, 4):
        for e in range(n_yh):
            if by or e:
                pl.semaphore_signal(barrier, inc=1, device_id=(ctx_at(by), yh_at(e) * n_x + x), device_id_type=MESH)
                count += 1
    for d in range(1, n_x):
        for e in range(n_yh):
            pl.semaphore_signal(barrier, inc=1, device_id=(c, yh_at(e) * n_x + x_at(d)), device_id_type=MESH)
            count += 1
    for d in range(1, n_z):
        pl.semaphore_signal(barrier, inc=1, device_id=(z_at(d), h), device_id_type=MESH)
        count += 1

    loads = [
        near(doc_hbm.at[c], doc, load_sem.at[0]),
        near(rope_hbm, rope, load_sem.at[1]),
        near(lat_hbm, keys.at[pl.ds(own, tok), pl.ds(0, wid)], load_sem.at[2]),
        near(qr_hbm, qr, load_sem.at[3]),
        near(q_hbm, qx.at[:, pl.ds(0, wid)], load_sem.at[4]),
        near(og_hbm, og, load_sem.at[5]),
        near(in_hbm, inp.at[0], load_sem.at[6]),
    ]
    for copy in loads:
        copy.start()

    n_rope = rope.shape[0]
    loads[0].wait()
    loads[1].wait()
    ids = doc[...]
    lane_t = iota((EXT, tok), 0)
    here_t = (lane_t - n_rope == ids).astype(F32).astype(BF16)
    tag_rows = (lane_t >= n_rope) & (lane_t < n_rope + 8)
    away_t = jnp.where(tag_rows & (lane_t - n_rope != ids), FAR, 0.0).astype(BF16)
    eye = (iota((tok, tok), 0) == iota((tok, tok), 1)).astype(F32).astype(BF16)
    here = dot(eye, here_t, NT).astype(BF16)
    tagged = jnp.concatenate([rope[...].astype(F32), away_t[n_rope:].astype(F32)], axis=0).astype(BF16)
    keys[pl.ds(own, tok), pl.ds(wid, EXT)] = dot(eye, tagged, NT).astype(BF16)
    loads[2].wait()

    pl.semaphore_wait(barrier, count)
    halo = [
        send(keys.at[pl.ds(own, tok)], keys.at[pl.ds((3 - by) * tok, tok)], hs_sem.at[by - 1], hr_sem.at[by - 1],
             ctx_at(by), h)
        for by in (3, 2, 1)
    ]

    step = min(rows, 128)
    per = step // heads
    cols = heads * n_rope
    spread = (lax.div(iota((step, per), 0), heads) == iota((step, per), 1)).astype(F32).astype(BF16)
    gather = (lax.div(iota((per, step), 1), heads) == iota((per, step), 0)).astype(F32).astype(BF16)
    head_of = (lax.div(iota((step, cols), 1), n_rope) == lax.rem(iota((step, cols), 0), heads)).astype(F32)
    hot[...] = here
    pick[...] = (lax.rem(iota((cols, EXT), 0), n_rope) == iota((cols, EXT), 1)).astype(F32).astype(BF16)
    drop[...] = (lax.rem(iota((EXT, cols), 1), n_rope) == iota((EXT, cols), 0)).astype(F32).astype(BF16)
    line, place_of = iota((wid, wid), 0), iota((wid, wid), 1)
    target = lax.rem(lax.div(line, 8), n_z) * (8 * QUAD) + lax.div(line, 8 * n_z) * 8 + lax.rem(line, 8)
    perm[...] = (target == place_of).astype(F32).astype(BF16)
    loads[3].wait()

    @pl.loop(0, rows // step)
    def _(i):
        ts = pl.ds(pl.multiple_of(i * per, per), per)
        rs = pl.ds(pl.multiple_of(i * step, step), step)
        wide = (dot(spread, qr[ts, :]) * head_of).astype(BF16)
        qx[rs, pl.ds(wid, EXT)] = (dot(wide, pick[...]) + dot(spread, hot[ts, :])).astype(BF16)

    loads[4].wait()
    loads[5].wait()
    big = min(rows, 256)

    def score(k0, k1):
        @pl.loop(0, rows // big)
        def _(i):
            rs = pl.ds(pl.multiple_of(i * big, big), big)
            st[pl.ds(k0, k1 - k0), rs] = dot(keys[pl.ds(k0, k1 - k0), :], qx[rs, :], NT)
            dt[pl.ds(k0, k1 - k0), rs] = dot(keys[pl.ds(k0, k1 - k0), pl.ds(0, wid)], og[rs, :], NT)

    score(own, own + tok)
    for copy in halo:
        copy.wait_recv()
    loads[6].wait()
    swap = [send(inp.at[0], inp.at[d], is_sem.at[d - 1], ir_sem.at[d - 1], quad_at(d), h) for d in (1, 2, 3)]
    score(0, own)

    @pl.loop(0, rows // step)
    def _(i):
        rs = pl.ds(pl.multiple_of(i * step, step), step)
        row = iota((tok, step), 0)
        t = i * per + lax.div(iota((tok, step), 1), heads)
        first = jnp.where(row > t, st[pl.ds(0, tok), rs], FAR)
        last = jnp.where(row <= t, st[pl.ds(own, tok), rs], FAR)
        s = jnp.concatenate([first, st[pl.ds(tok, own - tok), rs], last], axis=0) * SCALE
        e = jnp.exp(s - jnp.max(s, axis=0, keepdims=True))
        p = e * (1.0 / jnp.sum(e, axis=0, keepdims=True))
        low = p.astype(BF16)
        dp = dt[:, rs]
        delta = jnp.sum(low.astype(F32) * dp, axis=0, keepdims=True)
        probs[:, rs] = low
        dscore[:, rs] = (p * (dp - delta) * SCALE).astype(BF16)

    x_sends = []
    for k, (c0, cc) in enumerate(chunks):
        at = pl.ds(c0, cc)
        total = dot(dscore[...], qx[:, at])
        if c0 < wid:
            total = total + dot(probs[...], og[:, at])
        total = total.astype(BF16).reshape(SLOTS, n_x, tok // n_x, cc)
        for xi in range(n_x):
            part[xi, :, :, at] = total[:, xi]
        x_sends.append([
            send(part.at[x_at(d), :, :, at], xbuf.at[d - 1, :, :, at], xs_sem.at[d - 1, k], xr_sem.at[d - 1, k],
                 c, yh * n_x + x_at(d))
            for d in range(1, n_x)
        ])

    @pl.loop(0, rows // step)
    def _(i):
        ts = pl.ds(pl.multiple_of(i * per, per), per)
        rs = pl.ds(pl.multiple_of(i * step, step), step)
        g = dot(dscore[:, rs], keys[...], TN)
        dq[rs, :] = g[:, :wid].astype(BF16)
        wide = (dot(g[:, wid:].astype(BF16), drop[...]) * head_of).astype(BF16)
        dqr[ts, :] = dot(gather, wide).astype(BF16)

    outs = [near(dq, dq_hbm, out_sem.at[0]), near(dqr, dqr_hbm, out_sem.at[1])]
    for copy in outs:
        copy.start()

    y_sends = []
    for k, (c0, cc) in enumerate(chunks):
        at = pl.ds(c0, cc)
        for copy in x_sends[k]:
            copy.wait_recv()
        total = part[x, :, :, at].astype(F32)
        for d in range(1, n_x):
            total = total + xbuf[d - 1, :, :, at].astype(F32)
        total = total.reshape(SLOTS, n_yh, 8, cc).astype(BF16)
        for yi in range(n_yh):
            ysend[yi, :, :, at] = total[:, yi]
        for s in range(SLOTS):
            for e in range(n_yh):
                if s < SLOTS - 1 or e:
                    y_sends.append(
                        send(ysend.at[yh_at(e), s, :, at], ybuf.at[s * n_yh + e, :, at], ys_sem.at[k, s * n_yh + e],
                             yr_sem.at[k, s * n_yh + e], ctx_at(s - 3), yh_at(e) * n_x + x))

    def all_of(k, group):
        size = (SLOTS * n_yh - 1)
        return group[k * size:(k + 1) * size]

    place_here = x * n_yh + yh
    g_sends = []
    for k, (c0, cc) in enumerate(chunks):
        at = pl.ds(c0, cc)
        for copy in all_of(k, y_sends):
            copy.wait_recv()
        total = ysend[yh, SLOTS - 1, :, at].astype(F32)
        for m in range(SLOTS * n_yh):
            if m != (SLOTS - 1) * n_yh:
                total = total + ybuf[m, :, at].astype(F32)
        gbuf[place_here, :, at] = total.astype(BF16)
        for d in range(n_x):
            for e in range(n_yh):
                if d or e:
                    g_sends.append(
                        send(gbuf.at[place_here, :, at], gbuf.at[place_here, :, at], gs_sem.at[k, d * n_yh + e],
                             gr_sem.at[k, d * n_yh + e], c, yh_at(e) * n_x + x_at(d)))

    def gathered(k):
        size = n_head - 1
        for copy in g_sends[k * size:(k + 1) * size]:
            copy.wait_recv()

    gathered(0)
    gathered(1)
    outs.append(near(gbuf.at[:, :, pl.ds(0, wid)], lg_hbm, out_sem.at[2]))
    outs[-1].start()
    whole = gbuf[:, :, pl.ds(0, wid)].astype(F32).reshape(tok, wid).astype(BF16)
    latp[...] = dot(perm[...], whole, NT).astype(BF16).reshape(QUAD, 8 * n_z, tok)
    e_sends = [
        send(latp.at[lax.rem(quad + d, QUAD)], ebuf.at[d - 1], es_sem.at[d - 1], er_sem.at[d - 1], quad_at(d), h)
        for d in (1, 2, 3)
    ]
    total = dot(latp[quad], inp[0], NT)
    for d in (1, 2, 3):
        swap[d - 1].wait_recv()
        e_sends[d - 1].wait_recv()
        total = total + dot(ebuf[d - 1], inp[d], NT)
    zsend[...] = total.reshape(n_z, 8, total.shape[1]).astype(BF16)
    z_sends = [
        send(zsend.at[lax.rem(z + d, n_z)], zbuf.at[d - 1], zs_sem.at[d - 1], zr_sem.at[d - 1], z_at(d), h)
        for d in sorted(range(1, n_z), key=lambda d: -min(d, n_z - d))
    ]
    gathered(2)
    ext = gbuf[:, :, pl.ds(wid, EXT)].astype(F32).reshape(tok, EXT).astype(BF16)
    take = (iota((n_rope, EXT), 0) == iota((n_rope, EXT), 1)).astype(F32).astype(BF16)
    krx[...] = dot(take, ext, NT).astype(BF16)
    outs.append(near(krx, krg_hbm, out_sem.at[3]))
    outs[-1].start()
    total = zsend[z].astype(F32)
    for copy in z_sends:
        copy.wait_recv()
    for d in range(1, n_z):
        total = total + zbuf[d - 1].astype(F32)
    pg[...] = total
    outs.append(near(pg, pg_hbm, out_sem.at[4]))
    outs[-1].start()
    for copy in halo + swap + sum(x_sends, []) + y_sends + g_sends + e_sends + z_sends:
        copy.wait_send()
    for copy in outs:
        copy.wait()


def solution(mesh):
    n_ctx, n_head = mesh.shape["ctx"], mesh.shape["head"]
    n_x = 4 if n_head == 16 else 2
    n_yh = n_head // n_x
    n_z = n_ctx // QUAD

    def shards(q_latent, q_rope, latent, key_rope, out_grad, inputs, doc_ids):
        tok, heads, wid = q_latent.shape
        n_rope, dloc = key_rope.shape[1], inputs.shape[1]
        rows, full, keys = tok * heads, wid + EXT, SLOTS * tok
        cfg = (n_ctx, n_z, n_yh, n_x, tok, wid, heads)
        vm = pltpu.VMEM
        dma = pltpu.SemaphoreType.DMA
        y_n = SLOTS * n_yh
        shape = jax.ShapeDtypeStruct
        anywhere = pl.BlockSpec(memory_space=pl.ANY)
        outs = pl.pallas_call(
            functools.partial(kernel, cfg),
            out_shape=(
                shape((rows, wid), BF16),
                shape((tok, heads * n_rope), BF16),
                shape((n_head, 8, wid), BF16),
                shape((n_rope, tok), BF16),
                shape((8, dloc), F32),
            ),
            in_specs=[anywhere] * 7,
            out_specs=(anywhere,) * 5,
            scratch_shapes=[
                vm((rows, full), BF16), vm((rows, wid), BF16), vm((tok, heads * n_rope), BF16),
                vm((keys, full), BF16), vm((n_rope, tok), BF16), vm((QUAD, dloc, tok), BF16),
                vm((1, tok), jnp.int32), vm((wid, wid), BF16),
                vm((keys, rows), F32), vm((keys, rows), F32), vm((keys, rows), BF16), vm((keys, rows), BF16),
                vm((n_x, SLOTS, tok // n_x, full), BF16), vm((n_x - 1, SLOTS, tok // n_x, full), BF16),
                vm((n_yh, SLOTS, 8, full), BF16), vm((y_n, 8, full), BF16),
                vm((n_head, 8, full), BF16), vm((QUAD, 8 * n_z, tok), BF16), vm((QUAD - 1, 8 * n_z, tok), BF16),
                vm((n_z, 8, dloc), BF16), vm((n_z - 1, 8, dloc), BF16),
                vm((rows, wid), BF16), vm((tok, heads * n_rope), BF16), vm((n_rope, tok), BF16),
                vm((8, dloc), F32), vm((tok, EXT), BF16), vm((heads * n_rope, EXT), BF16), vm((EXT, heads * n_rope), BF16),
                dma((7,)), dma((3,)), dma((3,)), dma((n_x - 1, 3)), dma((n_x - 1, 3)), dma((3, y_n)), dma((3, y_n)),
                dma((3, n_head)), dma((3, n_head)), dma((3,)), dma((3,)), dma((3,)), dma((3,)),
                dma((n_z - 1,)), dma((n_z - 1,)), dma((5,)),
            ],
            compiler_params=pltpu.CompilerParams(collective_id=0, has_side_effects=True),
            name="step",
        )(
            q_latent.reshape(rows, wid), q_rope, latent, key_rope.T, out_grad.reshape(rows, wid), inputs.T,
            doc_ids.reshape(n_ctx, 1, tok),
        )
        return (outs[0].reshape(tok, heads, wid), outs[1], outs[2].reshape(tok, wid), outs[3].T, outs[4])

    return jax.shard_map(
        shards,
        mesh=mesh,
        in_specs=(P("ctx", "head", None), P("ctx", "head"), P("ctx", None), P("ctx", None), P("ctx", "head", None),
                  P("ctx", "head"), P()),
        out_specs=(P("ctx", "head", None), P("ctx", "head"), P("ctx", None), P("ctx", None), P("ctx", "head")),
        check_vma=False,
    )
```

time: 287 us -> 81.8 us (0.29)
  the two profiles are of different devices: /device:TPU:8 before, /device:TPU:1 now
where the time goes in v1:
time: 81.8 us; the launch traced here: 81.5 us
  Pallas kernels  75.6 us (92%)
  local copies, waits for them, and re-layouts  5.3 us (6%)
    pallas_call x1, Pallas kernels, shards(): pl.pallas_call(functools.partial(kernel, cfg), out_shape=(shape((rows, wi...  75.6 us
    unnamed x13, local copies, waits for them, and re-layouts  5.3 us

profile of v1, /device:TPU:1, one launch (start us, length us, event | category | flops | bytes accessed | tf_op | source)
XLA Modules:
  0.0 81.5 jit_solution(5034560366549289591)
XLA Ops:
  0.6 75.6 %step.1 = (bf16[1024,512]{1,0:T(8,128)(2,1)}, bf16[128,512]{1,0:T(8,128)(2,1)}, bf16[16,8,512]{2,1,0:T(8,128)(2,1)}, bf16[64,128]{1,0:T(8,128)(2,1)}, f32[8,448]{1,0:T(8,128)}) custom-call(bf16[1024,512]{1,0:T(8,128)(2,1)} %bitcast.8, bf16[128,512]{1,0:T(8,128)(2,1)} %qr_hbm.1, bf16[128,512]{1,0:T(8,128)(2,1)} %lat_hbm.1, bf16[64,128]{1,0:T(8,128)(2,1)} %bitcast.14, ...), custom_call_target="tpu_custom_call" | custom-call | tf_op jit(solution)/shard_map/step/pallas_call | solution.py:302
  76.2 0.0 copy-start.1
  76.2 2.3 %copy.17 = bf16[128,8,512]{2,1,0:T(8,128)(2,1)} copy(bf16[128,8,512]{2,1,0:T(8,128)(2,1)} %bitcast.10) | data formatting | bytes 2097152
  78.5 0.0 copy-done.1
  78.5 0.0 copy-start
  78.5 0.7 copy.18
  79.2 0.3 copy-done
  79.5 0.0 copy-start.3
  79.5 0.7 copy.19
  80.1 0.1 copy-done.3
  80.2 0.0 copy-start.2
  80.2 0.6 copy.20
  80.8 0.1 copy-done.2
  80.9 0.6 copy.21
Async XLA Ops:
  76.2 2.3 %copy-start.1 = (bf16[128,512]{1,0:T(8,128)(2,1)S(1)}, bf16[128,512]{1,0:T(8,128)(2,1)}, u32[]{:S(2)}) copy-start(bf16[128,512]{1,0:T(8,128)(2,1)} %get-tuple-element.21) | copy-start | bytes 393220
  78.5 1.0 %copy-start = (bf16[16,8,512]{2,1,0:T(8,128)(2,1)S(1)}, bf16[16,8,512]{2,1,0:T(8,128)(2,1)}, u32[]{:S(2)}) copy-start(bf16[16,8,512]{2,1,0:T(8,128)(2,1)} %get-tuple-element.12) | copy-start | bytes 393220
  79.5 0.7 copy-start.3
  80.2 0.7 copy-start.2

commit v2 on v1

v2 whole, which is shorter than its diff:
```python
import functools

import jax
import jax.numpy as jnp
from jax import lax
from jax.experimental import pallas as pl
from jax.experimental.pallas import tpu as pltpu
from jax.sharding import PartitionSpec as P

MESH = pl.DeviceIdType.MESH
BF16, F32 = jnp.bfloat16, jnp.float32
SCALE = 192.0 ** (-0.5)
FAR = -1e30
EXT = 128
QUAD = 4
SLOTS = 4
NT = (((1,), (1,)), ((), ()))
TN = (((0,), (0,)), ((), ()))


def dot(a, b, dims=(((1,), (0,)), ((), ()))):
    return lax.dot_general(a, b, dims, preferred_element_type=F32)


def iota(shape, dim):
    return lax.broadcasted_iota(jnp.int32, shape, dim)


def kernel(cfg, q_hbm, qr_hbm, lat_hbm, rope_hbm, og_hbm, in_hbm, doc_hbm,
           dq, dqr, lg_out, krx, pg_out,
           qx, og, qr, keys, rope, inp, doc, perm, st, dt, weights, both, part, xbuf, ysend, ybuf,
           gbuf, tbuf, zsend, zbuf, hot, pick, drop,
           load_sem, hs_sem, hr_sem, xs_sem, xr_sem, ys_sem, yr_sem, gs_sem, gr_sem,
           ts_sem, tr_sem, is_sem, ir_sem, zs_sem, zr_sem):
    n_ctx, n_z, n_yh, n_x, tok, wid, heads = cfg
    rows = tok * heads
    n_head = n_yh * n_x
    full = wid + EXT
    c, h = lax.axis_index("ctx"), lax.axis_index("head")
    z, quad = lax.div(c, QUAD), lax.rem(c, QUAD)
    yh, x = lax.div(h, n_x), lax.rem(h, n_x)
    own = (SLOTS - 1) * tok
    y_n = SLOTS * n_yh
    chunks = [(0, wid // 2), (wid // 2, wid // 2), (wid, EXT)]

    def ctx_at(by):
        return lax.rem(c + (by + n_ctx), n_ctx)

    def yh_at(by):
        return lax.rem(yh + by, n_yh)

    def x_at(by):
        return lax.rem(x + by, n_x)

    def quad_at(by):
        return z * QUAD + lax.rem(quad + by, QUAD)

    def z_at(by):
        return lax.rem(z + by, n_z) * QUAD + quad

    def near(ref_a, ref_b, sem):
        return pltpu.make_async_copy(ref_a, ref_b, sem)

    def send(src, dst, ssem, rsem, ci, hi):
        copy = pltpu.make_async_remote_copy(
            src_ref=src, dst_ref=dst, send_sem=ssem, recv_sem=rsem, device_id=(ci, hi), device_id_type=MESH
        )
        copy.start()
        return copy

    def group(ref, ssem, rsem):
        return pltpu.make_async_remote_copy(
            src_ref=ref, dst_ref=ref, send_sem=ssem, recv_sem=rsem, device_id=(c, h), device_id_type=MESH
        )

    barrier = pltpu.get_barrier_semaphore()
    count = 0
    for by in range(-3, 4):
        for e in range(n_yh):
            if by or e:
                pl.semaphore_signal(barrier, inc=1, device_id=(ctx_at(by), yh_at(e) * n_x + x), device_id_type=MESH)
                count += 1
    for d in range(1, n_x):
        for e in range(n_yh):
            pl.semaphore_signal(barrier, inc=1, device_id=(c, yh_at(e) * n_x + x_at(d)), device_id_type=MESH)
            count += 1
    for by in range(1, QUAD):
        for d in range(1, n_x):
            for e in range(n_yh):
                pl.semaphore_signal(
                    barrier, inc=1, device_id=(quad_at(by), yh_at(e) * n_x + x_at(d)), device_id_type=MESH)
                count += 1
    for d in range(1, n_z):
        pl.semaphore_signal(barrier, inc=1, device_id=(z_at(d), h), device_id_type=MESH)
        count += 1

    loads = [
        near(doc_hbm.at[c], doc, load_sem.at[0]),
        near(rope_hbm, rope, load_sem.at[1]),
        near(lat_hbm, keys.at[pl.ds(own, tok), pl.ds(0, wid)], load_sem.at[2]),
        near(qr_hbm, qr, load_sem.at[3]),
        near(q_hbm, qx.at[:, pl.ds(0, wid)], load_sem.at[4]),
        near(og_hbm, og, load_sem.at[5]),
        near(in_hbm, inp.at[0], load_sem.at[6]),
    ]
    for copy in loads:
        copy.start()

    n_rope = rope.shape[0]
    loads[0].wait()
    loads[1].wait()
    ids = doc[...]
    lane_t = iota((EXT, tok), 0)
    here_t = (lane_t - n_rope == ids).astype(F32).astype(BF16)
    tag_rows = (lane_t >= n_rope) & (lane_t < n_rope + 8)
    away_t = jnp.where(tag_rows & (lane_t - n_rope != ids), FAR, 0.0).astype(BF16)
    eye = (iota((tok, tok), 0) == iota((tok, tok), 1)).astype(F32).astype(BF16)
    here = dot(eye, here_t, NT).astype(BF16)
    tagged = jnp.concatenate([rope[...].astype(F32), away_t[n_rope:].astype(F32)], axis=0).astype(BF16)
    keys[pl.ds(own, tok), pl.ds(wid, EXT)] = dot(eye, tagged, NT).astype(BF16)
    loads[2].wait()

    pl.semaphore_wait(barrier, count)
    core = lax.rem(c, 2)
    side = pl.multiple_of((2 - 2 * core) * tok, tok)
    halo = [
        send(keys.at[pl.ds(own, tok)], keys.at[pl.ds(tok, tok)], hs_sem.at[0], hr_sem.at[0], ctx_at(2), h),
        send(keys.at[pl.ds(own, tok)], keys.at[pl.ds(side, tok)], hs_sem.at[1], hr_sem.at[1], ctx_at(1 + 2 * core), h),
    ]

    step = min(rows, 128)
    per = step // heads
    cols = heads * n_rope
    spread = (lax.div(iota((step, per), 0), heads) == iota((step, per), 1)).astype(F32).astype(BF16)
    gather = (lax.div(iota((per, step), 1), heads) == iota((per, step), 0)).astype(F32).astype(BF16)
    head_of = (lax.div(iota((step, cols), 1), n_rope) == lax.rem(iota((step, cols), 0), heads)).astype(F32)
    hot[...] = here
    pick[...] = (lax.rem(iota((cols, EXT), 0), n_rope) == iota((cols, EXT), 1)).astype(F32).astype(BF16)
    drop[...] = (lax.rem(iota((EXT, cols), 1), n_rope) == iota((EXT, cols), 0)).astype(F32).astype(BF16)
    line, place_of = iota((wid, wid), 0), iota((wid, wid), 1)
    target = lax.rem(lax.div(line, 8), n_z) * (8 * QUAD) + lax.div(line, 8 * n_z) * 8 + lax.rem(line, 8)
    perm[...] = (target == place_of).astype(F32).astype(BF16)
    loads[3].wait()

    @pl.loop(0, rows // step)
    def _(i):
        ts = pl.ds(pl.multiple_of(i * per, per), per)
        rs = pl.ds(pl.multiple_of(i * step, step), step)
        wide = (dot(spread, qr[ts, :]) * head_of).astype(BF16)
        qx[rs, pl.ds(wid, EXT)] = (dot(wide, pick[...]) + dot(spread, hot[ts, :])).astype(BF16)

    loads[4].wait()
    loads[5].wait()
    big = min(rows, 256)

    @pl.loop(0, rows // big)
    def _(i):
        rs = pl.ds(pl.multiple_of(i * big, big), big)
        low = pl.ds(pl.multiple_of(i * big + rows, big), big)
        both[rs, pl.ds(0, wid)] = dot(qx[rs, pl.ds(0, wid)], perm[...], NT).astype(BF16)
        both[rs, pl.ds(wid, EXT)] = qx[rs, pl.ds(wid, EXT)]
        both[low, pl.ds(0, wid)] = dot(og[rs, :], perm[...], NT).astype(BF16)

    def score(k0, k1, rs):
        st[pl.ds(k0, k1 - k0), rs] = dot(keys[pl.ds(k0, k1 - k0), :], qx[rs, :], NT)
        dt[pl.ds(k0, k1 - k0), rs] = dot(keys[pl.ds(k0, k1 - k0), pl.ds(0, wid)], og[rs, :], NT)

    @pl.loop(0, rows // big)
    def _(i):
        score(own, own + tok, pl.ds(pl.multiple_of(i * big, big), big))

    halo[0].wait_recv()
    across = pl.multiple_of(2 * core * tok, tok)
    halo.append(
        send(keys.at[pl.ds(tok, tok)], keys.at[pl.ds(across, tok)], hs_sem.at[2], hr_sem.at[2], ctx_at(1 - 2 * core), h))
    loads[6].wait()
    for copy in halo[1:]:
        copy.wait_recv()
    swap = [send(inp.at[0], inp.at[d], is_sem.at[d - 1], ir_sem.at[d - 1], quad_at(d), h) for d in (1, 2, 3)]
    def soft(i):
        rs = pl.ds(i * step, step)
        row = iota((tok, step), 0)
        t = i * per + lax.div(iota((tok, step), 1), heads)
        first = jnp.where(row > t, st[pl.ds(0, tok), rs], FAR)
        last = jnp.where(row <= t, st[pl.ds(own, tok), rs], FAR)
        s = jnp.concatenate([first, st[pl.ds(tok, own - tok), rs], last], axis=0)
        e = jnp.exp((s - jnp.max(s, axis=0, keepdims=True)) * SCALE)
        p = e * (1.0 / jnp.sum(e, axis=0, keepdims=True))
        low = p.astype(BF16)
        dp = dt[:, rs]
        delta = jnp.sum(low.astype(F32) * dp, axis=0, keepdims=True)
        weights[:, pl.ds(rows + i * step, step)] = low
        weights[:, rs] = (p * (dp - delta) * SCALE).astype(BF16)

    parts = big // step
    for i in range(rows // big + 1):
        if i < rows // big:
            score(0, own, pl.ds(i * big, big))
        if i:
            for m in range(parts):
                soft((i - 1) * parts + m)

    for k, (c0, cc) in enumerate(chunks):
        at = pl.ds(c0, cc)
        deep = pl.ds(0, 2 * rows if c0 < wid else rows)
        total = dot(weights[:, deep], both[deep, at])
        total = total.astype(BF16).reshape(SLOTS, n_x, tok // n_x, cc)
        for xi in range(n_x):
            part[xi, :, :, at] = total[:, xi]
        for d in range(1, n_x):
            send(part.at[x_at(d), :, :, at], xbuf.at[d - 1, :, :, at], xs_sem, xr_sem.at[k],
                 c, yh * n_x + x_at(d))

    def query_grads(i):
        ts = pl.ds(pl.multiple_of(i * per, per), per)
        rs = pl.ds(pl.multiple_of(i * step, step), step)
        g = dot(weights[:, rs], keys[...], TN)
        dq[rs, :] = g[:, :wid].astype(BF16)
        wide = (dot(g[:, wid:].astype(BF16), drop[...]) * head_of).astype(BF16)
        dqr[ts, :] = dot(gather, wide).astype(BF16)

    early = rows // step * 5 // 8
    pl.loop(0, early)(query_grads)

    for k, (c0, cc) in enumerate(chunks):
        at = pl.ds(c0, cc)
        group(xbuf.at[:, :, :, at], xs_sem, xr_sem.at[k]).wait_recv()
        total = part[x, :, :, at].astype(F32)
        for d in range(1, n_x):
            total = total + xbuf[d - 1, :, :, at].astype(F32)
        total = total.reshape(SLOTS, n_yh, 8, cc).astype(BF16)
        for yi in range(n_yh):
            ysend[yi, :, :, at] = total[:, yi]
        for s in range(SLOTS):
            for e in range(n_yh):
                if s < SLOTS - 1 or e:
                    send(ysend.at[yh_at(e), s, :, at], ybuf.at[(s * n_yh + e + n_yh) % y_n, :, at], ys_sem, yr_sem.at[k],
                         ctx_at(s - 3), yh_at(e) * n_x + x)

    pl.loop(early, rows // step)(query_grads)
    place_here = x * n_yh + yh
    def settle(k):
        at = pl.ds(*chunks[k])
        group(ybuf.at[pl.ds(1, y_n - 1), :, at], ys_sem, yr_sem.at[k]).wait_recv()
        total = ysend[yh, SLOTS - 1, :, at].astype(F32)
        total = total + jnp.sum(ybuf[pl.ds(1, y_n - 1), :, at].astype(F32), axis=0)
        gbuf[place_here, :, at] = total.astype(BF16)

    def spread_out(k):
        at = pl.ds(*chunks[k])
        for d in range(n_x):
            for e in range(n_yh):
                if d or e:
                    send(gbuf.at[place_here, :, at], gbuf.at[place_here, :, at], gs_sem, gr_sem.at[k],
                         c, yh_at(e) * n_x + x_at(d))

    quarter = wid // QUAD
    for k in (0, 1):
        settle(k)
        for to in (2 * k, 2 * k + 1):
            piece = gbuf.at[place_here, :, pl.ds(to * quarter, quarter)]
            by = lax.rem(to + QUAD - quad, QUAD)
            spot = tbuf.at[by * n_head + place_here]
            for d in reversed(range(n_x)):
                for e in reversed(range(n_yh)):
                    if d or e:
                        send(piece, spot, ts_sem, tr_sem, z * QUAD + to, yh_at(e) * n_x + x_at(d))

            @pl.when(quad != to)
            def _():
                send(piece, spot, ts_sem, tr_sem, z * QUAD + to, h)

            @pl.when(quad == to)
            def _():
                tbuf[place_here] = gbuf[place_here, :, pl.ds(to * quarter, quarter)]

    spread_out(0)
    spread_out(1)
    settle(2)
    spread_out(2)
    for copy in swap:
        copy.wait_recv()
    t_all = tbuf.at[pl.ds(0, QUAD * n_head - 1)]
    group(t_all, ts_sem, tr_sem).wait_recv()
    square = tbuf[...].astype(F32).reshape(QUAD * tok, quarter).astype(BF16)
    turned = dot((iota((quarter, quarter), 0) == iota((quarter, quarter), 1)).astype(F32).astype(BF16), square, NT)
    turned = turned.astype(BF16)
    total = dot(turned[:, :tok], inp[0], NT)
    for d in (1, 2, 3):
        total = total + dot(turned[:, d * tok:(d + 1) * tok], inp[d], NT)
    zsend[...] = total.reshape(n_z, 8, total.shape[1]).astype(BF16)
    for d in sorted(range(1, n_z), key=lambda d: -min(d, n_z - d)):
        send(zsend.at[lax.rem(z + d, n_z)], zbuf.at[d - 1], zs_sem, zr_sem, z_at(d), h)
    for k in range(3):
        group(gbuf.at[pl.ds(0, n_head - 1), :, pl.ds(*chunks[k])], gs_sem, gr_sem.at[k]).wait_recv()
    whole = gbuf[...].astype(F32).reshape(tok, full).astype(BF16)
    lg_out[...] = dot(whole[:, :wid], perm[...]).astype(BF16)
    take = (iota((n_rope, EXT), 0) == iota((n_rope, EXT), 1)).astype(F32).astype(BF16)
    krx[...] = dot(take, whole[:, wid:], NT).astype(BF16)
    total = zsend[z].astype(F32)
    for k, (c0, cc) in enumerate(chunks):
        at = pl.ds(c0, cc)
        group(xbuf.at[:, :, :, at], xs_sem, xr_sem.at[k]).wait_send()
        group(ybuf.at[pl.ds(1, y_n - 1), :, at], ys_sem, yr_sem.at[k]).wait_send()
        group(gbuf.at[pl.ds(0, n_head - 1), :, at], gs_sem, gr_sem.at[k]).wait_send()
    group(t_all, ts_sem, tr_sem).wait_send()
    for copy in halo + swap:
        copy.wait_send()
    group(zbuf, zs_sem, zr_sem).wait_recv()
    total = total + jnp.sum(zbuf[...].astype(F32), axis=0)
    pg_out[...] = total
    group(zbuf, zs_sem, zr_sem).wait_send()


def flush(*refs):
    sem = refs[-1]
    copies = [pltpu.make_async_copy(refs[i], refs[i + 5], sem.at[i]) for i in range(5)]
    for copy in copies:
        copy.start()
    for copy in copies:
        copy.wait()


def solution(mesh):
    n_ctx, n_head = mesh.shape["ctx"], mesh.shape["head"]
    n_x = 4 if n_head == 16 else 2
    n_yh = n_head // n_x
    n_z = n_ctx // QUAD

    def shards(q_latent, q_rope, latent, key_rope, out_grad, inputs, doc_ids):
        tok, heads, wid = q_latent.shape
        n_rope, dloc = key_rope.shape[1], inputs.shape[1]
        rows, full, keys = tok * heads, wid + EXT, SLOTS * tok
        cfg = (n_ctx, n_z, n_yh, n_x, tok, wid, heads)
        vm = pltpu.VMEM
        dma = pltpu.SemaphoreType.DMA
        y_n = SLOTS * n_yh
        shape = jax.ShapeDtypeStruct
        anywhere, local = pl.BlockSpec(memory_space=pltpu.HBM), pl.BlockSpec(memory_space=pltpu.VMEM)
        shapes = (
                shape((rows, wid), BF16),
                shape((tok, heads * n_rope), BF16),
                shape((tok, wid), BF16),
                shape((n_rope, tok), BF16),
                shape((8, dloc), F32),
            )
        outs = pl.pallas_call(
            functools.partial(kernel, cfg),
            out_shape=shapes,
            in_specs=[pl.BlockSpec(memory_space=pltpu.HBM)] * 7,
            out_specs=(local,) * 5,
            scratch_shapes=[
                vm((rows, full), BF16), vm((rows, wid), BF16), vm((tok, heads * n_rope), BF16),
                vm((keys, full), BF16), vm((n_rope, tok), BF16), vm((QUAD, dloc, tok), BF16),
                vm((1, tok), jnp.int32), vm((wid, wid), BF16),
                vm((keys, rows), F32), vm((keys, rows), F32), vm((keys, 2 * rows), BF16), vm((2 * rows, full), BF16),
                vm((n_x, SLOTS, tok // n_x, full), BF16), vm((n_x - 1, SLOTS, tok // n_x, full), BF16),
                vm((n_yh, SLOTS, 8, full), BF16), vm((y_n, 8, full), BF16),
                vm((n_head, 8, full), BF16), vm((QUAD * n_head, 8, wid // QUAD), BF16),
                vm((n_z, 8, dloc), BF16), vm((n_z - 1, 8, dloc), BF16),
                vm((tok, EXT), BF16), vm((heads * n_rope, EXT), BF16), vm((EXT, heads * n_rope), BF16),
                dma((7,)), dma((3,)), dma((3,)), dma, dma((3,)), dma, dma((3,)), dma, dma((3,)),
                dma, dma, dma((3,)), dma((3,)), dma, dma,
            ],
            compiler_params=pltpu.CompilerParams(collective_id=0, has_side_effects=True, vmem_limit_bytes=54_000_000),
            name="step",
        )(
            q_latent.reshape(rows, wid), q_rope, latent, key_rope.T, out_grad.reshape(rows, wid), inputs.T,
            doc_ids.reshape(n_ctx, 1, tok),
        )
        outs = pl.pallas_call(
            flush,
            out_shape=shapes,
            in_specs=[local] * 5,
            out_specs=(anywhere,) * 5,
            scratch_shapes=[dma((5,))],
            compiler_params=pltpu.CompilerParams(vmem_limit_bytes=2 << 20),
            name="flush",
        )(*outs)
        return (outs[0].reshape(tok, heads, wid), outs[1], outs[2], outs[3].T, outs[4])

    return jax.shard_map(
        shards,
        mesh=mesh,
        in_specs=(P("ctx", "head", None), P("ctx", "head"), P("ctx", None), P("ctx", None), P("ctx", "head", None),
                  P("ctx", "head"), P()),
        out_specs=(P("ctx", "head", None), P("ctx", "head"), P("ctx", None), P("ctx", None), P("ctx", "head")),
        check_vma=False,
    )
```

time: 81.8 us -> 69.8 us (0.85)
  the two profiles are of different devices: /device:TPU:1 before, /device:TPU:8 now
where the time goes in v2:
time: 69.8 us; the launch traced here: 69.2 us
  Pallas kernels  64.4 us (92%)
  local copies, waits for them, and re-layouts  4.17 us (6%)
    pallas_call x1, Pallas kernels, shards(): pl.pallas_call(functools.partial(kernel, cfg), out_shape=shapes, in_specs...  63.3 us
    unnamed x10, local copies, waits for them, and re-layouts  4.17 us

profile of v2, /device:TPU:8, one launch (start us, length us, event | category | flops | bytes accessed | tf_op | source)
XLA Modules:
  0.0 69.2 jit_solution(5956266497841069572)
XLA Ops:
  0.6 0.0 copy-start
  0.6 0.9 %copy-done = bf16[128,512]{1,0:T(8,128)(2,1)S(1)} copy-done((bf16[128,512]{1,0:T(8,128)(2,1)S(1)}, bf16[128,512]{1,0:T(8,128)(2,1)}, u32[]{:S(2)}) %copy-start) | copy-done | bytes 131096
  1.5 0.0 copy-start.1
  1.5 0.9 %copy-done.1 = bf16[128,512]{1,0:T(8,128)(2,1)S(1)} copy-done((bf16[128,512]{1,0:T(8,128)(2,1)S(1)}, bf16[128,512]{1,0:T(8,128)(2,1)}, u32[]{:S(2)}) %copy-start.1) | copy-done | bytes 131096
  2.4 0.0 copy-start.2
  2.4 0.9 %copy-done.2 = bf16[128,448]{0,1:T(8,128)(2,1)S(1)} copy-done((bf16[128,448]{0,1:T(8,128)(2,1)S(1)}, bf16[128,448]{0,1:T(8,128)(2,1)}, u32[]{:S(2)}) %copy-start.2) | copy-done | bytes 114712
  3.3 0.0 copy-start.3
  3.3 0.8 %copy-done.3 = s32[8192]{0:T(1024)S(1)} copy-done((s32[8192]{0:T(1024)S(1)}, s32[8192]{0:T(1024)}, u32[]{:S(2)}) %copy-start.3) | copy-done | bytes 32792
  4.1 0.0 copy-start.4
  4.1 0.7 %copy-done.4 = bf16[128,64]{0,1:T(8,128)(2,1)S(1)} copy-done((bf16[128,64]{0,1:T(8,128)(2,1)S(1)}, bf16[128,64]{0,1:T(8,128)(2,1)}, u32[]{:S(2)}) %copy-start.4) | copy-done | bytes 16408
  4.8 63.3 %step.1 = (bf16[1024,512]{1,0:T(8,128)(2,1)S(1)}, bf16[128,512]{1,0:T(8,128)(2,1)S(1)}, bf16[128,512]{1,0:T(8,128)(2,1)S(1)}, bf16[64,128]{1,0:T(8,128)(2,1)S(1)}, f32[8,448]{1,0:T(8,128)S(1)}) custom-call(bf16[1024,512]{1,0:T(8,128)(2,1)} %bitcast.10, bf16[128,512]{1,0:T(8,128)(2,1)S(1)} %copy-done, bf16[128,512]{1,0:T(8,128)(2,1)S(1)} %copy-done.1, ...), custom_call_target="tpu_custom_call" | custom-call | tf_op jit(solution)/shard_map/step/pallas_call | solution.py:347
  68.1 1.1 %flush.1 = (bf16[1024,512]{1,0:T(8,128)(2,1)}, bf16[128,512]{1,0:T(8,128)(2,1)}, bf16[128,512]{1,0:T(8,128)(2,1)}, bf16[64,128]{1,0:T(8,128)(2,1)}, f32[8,448]{1,0:T(8,128)}) custom-call(bf16[1024,512]{1,0:T(8,128)(2,1)S(1)} %get-tuple-element.15.refs_0_, bf16[128,512]{1,0:T(8,128)(2,1)S(1)} %get-tuple-element.16.refs_1_, ...), custom_call_target="tpu_custom_call" | custom-call | tf_op jit(solution)/shard_map/flush/pallas_call | solution.py:371
Async XLA Ops:
  0.6 0.9 %copy-start = (bf16[128,512]{1,0:T(8,128)(2,1)S(1)}, bf16[128,512]{1,0:T(8,128)(2,1)}, u32[]{:S(2)}) copy-start(bf16[128,512]{1,0:T(8,128)(2,1)} %qr_hbm.1) | copy-start | bytes 393220
  1.5 0.9 %copy-start.1 = (bf16[128,512]{1,0:T(8,128)(2,1)S(1)}, bf16[128,512]{1,0:T(8,128)(2,1)}, u32[]{:S(2)}) copy-start(bf16[128,512]{1,0:T(8,128)(2,1)} %lat_hbm.1) | copy-start | bytes 393220
  2.4 0.9 %copy-start.2 = (bf16[128,448]{0,1:T(8,128)(2,1)S(1)}, bf16[128,448]{0,1:T(8,128)(2,1)}, u32[]{:S(2)}) copy-start(bf16[128,448]{0,1:T(8,128)(2,1)} %param.12) | copy-start | bytes 344068
  3.3 0.8 %copy-start.3 = (s32[8192]{0:T(1024)S(1)}, s32[8192]{0:T(1024)}, u32[]{:S(2)}) copy-start(s32[8192]{0:T(1024)} %param.13) | copy-start | bytes 98308
  4.1 0.7 %copy-start.4 = (bf16[128,64]{0,1:T(8,128)(2,1)S(1)}, bf16[128,64]{0,1:T(8,128)(2,1)}, u32[]{:S(2)}) copy-start(bf16[128,64]{0,1:T(8,128)(2,1)} %param.10) | copy-start | bytes 49156

commit v3 on v2

--- a/solution.py
+++ b/solution.py
@@ -72,6 +72,18 @@
         return pltpu.make_async_remote_copy(
             src_ref=ref, dst_ref=ref, send_sem=ssem, recv_sem=rsem, device_id=(c, h), device_id_type=MESH
         )
+
+    loads = [
+        near(doc_hbm.at[c], doc, load_sem.at[0]),
+        near(rope_hbm, rope, load_sem.at[1]),
+        near(lat_hbm, keys.at[pl.ds(own, tok), pl.ds(0, wid)], load_sem.at[2]),
+        near(qr_hbm, qr, load_sem.at[3]),
+        near(q_hbm, qx.at[:, pl.ds(0, wid)], load_sem.at[4]),
+        near(og_hbm, og, load_sem.at[5]),
+        near(in_hbm, inp.at[0], load_sem.at[6]),
+    ]
+    for copy in loads:
+        copy.start()
 
     barrier = pltpu.get_barrier_semaphore()
     count = 0
@@ -94,18 +106,6 @@
         pl.semaphore_signal(barrier, inc=1, device_id=(z_at(d), h), device_id_type=MESH)
         count += 1
 
-    loads = [
-        near(doc_hbm.at[c], doc, load_sem.at[0]),
-        near(rope_hbm, rope, load_sem.at[1]),
-        near(lat_hbm, keys.at[pl.ds(own, tok), pl.ds(0, wid)], load_sem.at[2]),
-        near(qr_hbm, qr, load_sem.at[3]),
-        near(q_hbm, qx.at[:, pl.ds(0, wid)], load_sem.at[4]),
-        near(og_hbm, og, load_sem.at[5]),
-        near(in_hbm, inp.at[0], load_sem.at[6]),
-    ]
-    for copy in loads:
-        copy.start()
-
     n_rope = rope.shape[0]
     loads[0].wait()
     loads[1].wait()
@@ -153,6 +153,18 @@
     loads[5].wait()
     big = min(rows, 256)
 
+    def score(k0, k1, rs):
+        st[pl.ds(k0, k1 - k0), rs] = dot(keys[pl.ds(k0, k1 - k0), :], qx[rs, :], NT)
+        dt[pl.ds(k0, k1 - k0), rs] = dot(keys[pl.ds(k0, k1 - k0), pl.ds(0, wid)], og[rs, :], NT)
+
+    @pl.loop(0, rows // big)
+    def _(i):
+        score(own, own + tok, pl.ds(pl.multiple_of(i * big, big), big))
+
+    halo[0].wait_recv()
+    across = pl.multiple_of(2 * core * tok, tok)
+    halo.append(
+        send(keys.at[pl.ds(tok, tok)], keys.at[pl.ds(across, tok)], hs_sem.at[2], hr_sem.at[2], ctx_at(1 - 2 * core), h))
     @pl.loop(0, rows // big)
     def _(i):
         rs = pl.ds(pl.multiple_of(i * big, big), big)
@@ -161,18 +173,6 @@
         both[rs, pl.ds(wid, EXT)] = qx[rs, pl.ds(wid, EXT)]
         both[low, pl.ds(0, wid)] = dot(og[rs, :], perm[...], NT).astype(BF16)
 
-    def score(k0, k1, rs):
-        st[pl.ds(k0, k1 - k0), rs] = dot(keys[pl.ds(k0, k1 - k0), :], qx[rs, :], NT)
-        dt[pl.ds(k0, k1 - k0), rs] = dot(keys[pl.ds(k0, k1 - k0), pl.ds(0, wid)], og[rs, :], NT)
-
-    @pl.loop(0, rows // big)
-    def _(i):
-        score(own, own + tok, pl.ds(pl.multiple_of(i * big, big), big))
-
-    halo[0].wait_recv()
-    across = pl.multiple_of(2 * core * tok, tok)
-    halo.append(
-        send(keys.at[pl.ds(tok, tok)], keys.at[pl.ds(across, tok)], hs_sem.at[2], hr_sem.at[2], ctx_at(1 - 2 * core), h))
     loads[6].wait()
     for copy in halo[1:]:
         copy.wait_recv()
@@ -362,12 +362,13 @@
                 dma((7,)), dma((3,)), dma((3,)), dma, dma((3,)), dma, dma((3,)), dma, dma((3,)),
                 dma, dma, dma((3,)), dma((3,)), dma, dma,
             ],
-            compiler_params=pltpu.CompilerParams(collective_id=0, has_side_effects=True, vmem_limit_bytes=54_000_000),
+            compiler_params=pltpu.CompilerParams(collective_id=0, has_side_effects=True, vmem_limit_bytes=48 << 20),
             name="step",
-        )(
-            q_latent.reshape(rows, wid), q_rope, latent, key_rope.T, out_grad.reshape(rows, wid), inputs.T,
-            doc_ids.reshape(n_ctx, 1, tok),
-        )
+        )(*(
+            pltpu.with_memory_space_constraint(a, pltpu.HBM)
+            for a in (q_latent.reshape(rows, wid), q_rope, latent, key_rope.T, out_grad.reshape(rows, wid), inputs.T,
+                      doc_ids.reshape(n_ctx, 1, tok))
+        ))
         outs = pl.pallas_call(
             flush,
             out_shape=shapes,

time: 69.8 us -> 66.3 us (0.950)
  local copies, waits for them, and re-layouts: 4.17 us -> 0 us
  Pallas kernels: 64.4 us -> 65.4 us
    unnamed x10 -> x0, local copies, waits for them, and re-layouts: 4.17 us -> none
    pallas_call x1, Pallas kernels: 63.3 us -> 64.3 us  [shards(): pl.pallas_call(functools.partial(kernel, cfg), out_shape=shapes, in_specs...]
where the time goes in v3:
time: 66.3 us; the launch traced here: 66 us
  Pallas kernels  65.4 us (99%)
    pallas_call x1, Pallas kernels, shards(): pl.pallas_call(functools.partial(kernel, cfg), out_shape=shapes, in_specs...  64.3 us

profile of v3, /device:TPU:8, one launch (start us, length us, event | category | flops | bytes accessed | tf_op | source)
XLA Modules:
  0.0 66.0 jit_solution(1105564450337277859)
XLA Ops:
  0.6 64.3 %step.1 = (bf16[1024,512]{1,0:T(8,128)(2,1)S(1)}, bf16[128,512]{1,0:T(8,128)(2,1)S(1)}, bf16[128,512]{1,0:T(8,128)(2,1)S(1)}, bf16[64,128]{1,0:T(8,128)(2,1)S(1)}, f32[8,448]{1,0:T(8,128)S(1)}) custom-call(bf16[1024,512]{1,0:T(8,128)(2,1)} %bitcast.7, bf16[128,512]{1,0:T(8,128)(2,1)} %qr_hbm.1, bf16[128,512]{1,0:T(8,128)(2,1)} %lat_hbm.1, ...), custom_call_target="tpu_custom_call" | custom-call | tf_op jit(solution)/shard_map/step/pallas_call | solution.py:347
  64.9 1.1 %flush.1 = (bf16[1024,512]{1,0:T(8,128)(2,1)}, bf16[128,512]{1,0:T(8,128)(2,1)}, bf16[128,512]{1,0:T(8,128)(2,1)}, bf16[64,128]{1,0:T(8,128)(2,1)}, f32[8,448]{1,0:T(8,128)}) custom-call(bf16[1024,512]{1,0:T(8,128)(2,1)S(1)} %get-tuple-element.15.refs_0_, bf16[128,512]{1,0:T(8,128)(2,1)S(1)} %get-tuple-element.16.refs_1_, ...), custom_call_target="tpu_custom_call" | custom-call | tf_op jit(solution)/shard_map/flush/pallas_call | solution.py:372

commit v4 on v3

--- a/solution.py
+++ b/solution.py
@@ -219,8 +219,6 @@
         wide = (dot(g[:, wid:].astype(BF16), drop[...]) * head_of).astype(BF16)
         dqr[ts, :] = dot(gather, wide).astype(BF16)
 
-    early = rows // step * 5 // 8
-    pl.loop(0, early)(query_grads)
 
     for k, (c0, cc) in enumerate(chunks):
         at = pl.ds(c0, cc)
@@ -237,7 +235,6 @@
                     send(ysend.at[yh_at(e), s, :, at], ybuf.at[(s * n_yh + e + n_yh) % y_n, :, at], ys_sem, yr_sem.at[k],
                          ctx_at(s - 3), yh_at(e) * n_x + x)
 
-    pl.loop(early, rows // step)(query_grads)
     place_here = x * n_yh + yh
     def settle(k):
         at = pl.ds(*chunks[k])
@@ -276,8 +273,6 @@
 
     spread_out(0)
     spread_out(1)
-    settle(2)
-    spread_out(2)
     for copy in swap:
         copy.wait_recv()
     t_all = tbuf.at[pl.ds(0, QUAD * n_head - 1)]
@@ -291,6 +286,9 @@
     zsend[...] = total.reshape(n_z, 8, total.shape[1]).astype(BF16)
     for d in sorted(range(1, n_z), key=lambda d: -min(d, n_z - d)):
         send(zsend.at[lax.rem(z + d, n_z)], zbuf.at[d - 1], zs_sem, zr_sem, z_at(d), h)
+    settle(2)
+    spread_out(2)
+    pl.loop(0, rows // step)(query_grads)
     for k in range(3):
         group(gbuf.at[pl.ds(0, n_head - 1), :, pl.ds(*chunks[k])], gs_sem, gr_sem.at[k]).wait_recv()
     whole = gbuf[...].astype(F32).reshape(tok, full).astype(BF16)

time: 66.3 us -> 66.5 us (level)
  no operation moved by 1% of the time
where the time goes in v4:
time: 66.5 us; the launch traced here: 66.3 us
  Pallas kernels  65.7 us (99%)
    pallas_call x1, Pallas kernels, shards(): pl.pallas_call(functools.partial(kernel, cfg), out_shape=shapes, in_specs...  64.6 us

profile of v4, /device:TPU:8, one launch (start us, length us, event | category | flops | bytes accessed | tf_op | source)
XLA Modules:
  0.0 66.3 jit_solution(7701714172291923412)
XLA Ops:
  0.6 64.6 %step.1 = (bf16[1024,512]{1,0:T(8,128)(2,1)S(1)}, bf16[128,512]{1,0:T(8,128)(2,1)S(1)}, bf16[128,512]{1,0:T(8,128)(2,1)S(1)}, bf16[64,128]{1,0:T(8,128)(2,1)S(1)}, f32[8,448]{1,0:T(8,128)S(1)}) custom-call(bf16[1024,512]{1,0:T(8,128)(2,1)} %bitcast.7, bf16[128,512]{1,0:T(8,128)(2,1)} %qr_hbm.1, bf16[128,512]{1,0:T(8,128)(2,1)} %lat_hbm.1, ...), custom_call_target="tpu_custom_call" | custom-call | tf_op jit(solution)/shard_map/step/pallas_call | solution.py:345
  65.2 1.1 %flush.1 = (bf16[1024,512]{1,0:T(8,128)(2,1)}, bf16[128,512]{1,0:T(8,128)(2,1)}, bf16[128,512]{1,0:T(8,128)(2,1)}, bf16[64,128]{1,0:T(8,128)(2,1)}, f32[8,448]{1,0:T(8,128)}) custom-call(bf16[1024,512]{1,0:T(8,128)(2,1)S(1)} %get-tuple-element.15.refs_0_, bf16[128,512]{1,0:T(8,128)(2,1)S(1)} %get-tuple-element.16.refs_1_, ...), custom_call_target="tpu_custom_call" | custom-call | tf_op jit(solution)/shard_map/flush/pallas_call | solution.py:370
